TPU v7x, 32 devices: a whole 2x2x4 slice. The times are simulated.
32 devices in a mesh: pw: 8 (over z, core), band: 4 (over y, x).
Axes of the slice: x: 2, y: 2, z: 4, core: 2. Of those that a mesh axis runs over, the one named last changes fastest.
Arguments:
- wavefunctions: bfloat16 [2, 4096, 512], P(None, 'pw', 'band'), may hold values from -0.09375 to 0.09375
- miller: int32 [3, 4096], P(None, 'pw'), may hold values from -16 to 16
- reciprocal: float32 [3, 3], replicated, may hold values from -0.15 to 1.15, as said below
- fractional: float32 [3, 32], replicated, may hold values from 0 to 1
- species: int32 [32], replicated, may hold values from 0 to 3
- atom_order: int32 [32], replicated, may hold values from 0 to 31, each once
- radial_widths: float32 [4, 4], replicated, may hold values from 0.003 to 0.02
- onsite_base: float32 [4, 8, 8], replicated, may hold values from -2 to 2
- coupling: float32 [4, 64, 64], replicated, may hold values from -0.75 to 0.75
- occupations: float32 [512], P('band'), may hold values from 0 to 3, as said below
Outputs:
- applied: bfloat16 [2, 4096, 512], P(None, 'pw', 'band')
- onsite_d: float32 [32, 8, 8], P('pw')
Inputs may be any that keep to these rules, and one draw needn't show every extreme that they name: `atom_order`: a permutation of the atoms. `reciprocal`: each diagonal entry is 0.85 or more and each other entry 0.15 or less in magnitude. `occupations`: positive.
All inputs are finite; a program needn't handle non-finite values.
Results may differ from a plain program's by a relative error of at most 0.008.
Values may be sent and summed in bfloat16 or wider, within the bound.
A program may use at most 64 MiB of HBM per device.

v0:
```python
import math

import jax
import jax.numpy as jnp
from jax import lax
from jax.sharding import PartitionSpec as P

HIGH = lax.Precision.HIGHEST


def projector_tile(miller_cols, reciprocal, positions, atom_species, radial_widths):
    two_pi = 2.0 * math.pi
    miller_real = miller_cols.astype(jnp.float32)
    g_vectors = two_pi * jnp.dot(reciprocal, miller_real, precision=HIGH)
    g_square = jnp.sum(g_vectors * g_vectors, axis=0)
    phases = two_pi * jnp.dot(positions.T, miller_real, precision=HIGH)
    onehot = (
        atom_species[:, None] == jnp.arange(radial_widths.shape[0], dtype=jnp.int32)[None, :]
    ).astype(jnp.float32)
    widths = jnp.dot(onehot, radial_widths, precision=HIGH)
    radial = jnp.exp(-0.5 * g_square[None, None, :] * (widths * widths)[:, :, None])
    s_part = radial[:, 0:2, :]
    p_first = g_vectors[None, :, :] * (widths[:, 2, None, None] * radial[:, 2:3, :])
    p_second = g_vectors[None, :, :] * (widths[:, 3, None, None] * radial[:, 3:4, :])
    p_part = jnp.concatenate([p_first, p_second], axis=1)
    cosine = jnp.cos(phases)[:, None, :]
    sine = jnp.sin(phases)[:, None, :]
    beta_real = jnp.concatenate([s_part * cosine, -p_part * sine], axis=1)
    beta_imag = jnp.concatenate([-s_part * sine, -p_part * cosine], axis=1)
    rows = positions.shape[1] * 8
    return (
        beta_real.reshape(rows, -1).astype(jnp.bfloat16),
        beta_imag.reshape(rows, -1).astype(jnp.bfloat16),
    )


def project(beta_real, beta_imag, wave_real, wave_imag):
    proj_real = jnp.dot(beta_real, wave_real, preferred_element_type=jnp.float32) + jnp.dot(
        beta_imag, wave_imag, preferred_element_type=jnp.float32
    )
    proj_imag = jnp.dot(beta_real, wave_imag, preferred_element_type=jnp.float32) - jnp.dot(
        beta_imag, wave_real, preferred_element_type=jnp.float32
    )
    return jnp.stack([proj_real, proj_imag], axis=1)


def occupancy_terms(projections, weights):
    grouped = projections.reshape(projections.shape[0] // 8, 8, 2, projections.shape[2])
    return jnp.einsum("aicn,ajcn,n->aij", grouped, grouped, weights, precision=HIGH)


def onsite_matrix(occupancy, atom_species, onsite_base, coupling):
    holding = occupancy.shape[0]
    kinds = onsite_base.shape[0]
    onehot = (atom_species[:, None] == jnp.arange(kinds, dtype=jnp.int32)[None, :]).astype(
        jnp.float32
    )
    response = jnp.einsum("skl,al->ask", coupling, occupancy.reshape(holding, 64), precision=HIGH)
    base = jnp.einsum("as,sk->ak", onehot, onsite_base.reshape(kinds, 64), precision=HIGH)
    total = base + jnp.einsum("as,ask->ak", onehot, response, precision=HIGH)
    return total.reshape(holding, 8, 8)


def weigh(onsite, projections):
    grouped = projections.reshape(projections.shape[0] // 8, 8, 2, projections.shape[2])
    weighted = jnp.einsum("aij,ajcn->aicn", onsite, grouped, precision=HIGH)
    return weighted.reshape(projections.shape).astype(jnp.bfloat16)


def back_project(beta_real, beta_imag, weighted):
    dims = (((0,), (0,)), ((), ()))
    q_real = weighted[:, 0, :]
    q_imag = weighted[:, 1, :]
    out_real = lax.dot_general(
        beta_real, q_real, dims, preferred_element_type=jnp.float32
    ) - lax.dot_general(beta_imag, q_imag, dims, preferred_element_type=jnp.float32)
    out_imag = lax.dot_general(
        beta_real, q_imag, dims, preferred_element_type=jnp.float32
    ) + lax.dot_general(beta_imag, q_real, dims, preferred_element_type=jnp.float32)
    return jnp.stack([out_real, out_imag], axis=0)


def local(
    wavefunctions,
    miller,
    reciprocal,
    fractional,
    species,
    atom_order,
    radial_widths,
    onsite_base,
    coupling,
    occupations,
):
    sorted_species = species[atom_order]
    sorted_positions = fractional[:, atom_order]
    owned_atoms = atom_order.shape[0] // lax.axis_size("pw")
    owner_index = lax.axis_index("pw")
    weights = occupations / (occupations.shape[0] * lax.axis_size("band"))
    wave_real = wavefunctions[0]
    wave_imag = wavefunctions[1]
    positions = sorted_positions
    kinds = sorted_species
    beta_real, beta_imag = projector_tile(miller, reciprocal, positions, kinds, radial_widths)
    projections = lax.psum_scatter(
        project(beta_real, beta_imag, wave_real, wave_imag), "pw", scatter_dimension=0, tiled=True
    )
    own_species = lax.dynamic_slice_in_dim(
        sorted_species, owner_index * owned_atoms, owned_atoms, 0
    )
    occupancy = lax.psum(occupancy_terms(projections, weights), "band")
    onsite_own = onsite_matrix(occupancy, own_species, onsite_base, coupling)
    weighted = weigh(onsite_own, projections)
    positions = sorted_positions
    kinds = sorted_species
    beta_real, beta_imag = projector_tile(miller, reciprocal, positions, kinds, radial_widths)
    applied = back_project(beta_real, beta_imag, lax.all_gather(weighted, "pw", axis=0, tiled=True))
    return (applied.astype(jnp.bfloat16), onsite_own)


def solution(mesh):
    placed = (P(None, "pw", "band"), P(None, "pw"), P(), P(), P(), P(), P(), P(), P(), P("band"))
    return jax.shard_map(
        local,
        mesh=mesh,
        in_specs=placed,
        out_specs=(P(None, "pw", "band"), P("pw", None, None)),
        check_vma=False,
    )
```

profile of v0, /device:TPU:0, one launch (start us, length us, event | category | flops | bytes accessed | tf_op | source)
XLA Modules:
  0.0 84.7 jit_solution(17103418098538546727)
XLA Ops:
  7.2 0.7 compare_select_fusion
  7.9 0.6 copy-done.1
  8.6 0.7 gather_fusion
  9.5 0.5 copy-done.4
  10.5 0.6 copy-done.7
  11.1 0.6 gather_fusion.1
  11.7 0.4 fusion.35
  12.9 0.8 copy-done.3
  14.2 0.3 fusion.4
  14.5 0.3 fusion.5
  14.7 0.7 pad_maximum_fusion
  15.5 0.7 copy-done.5
  16.3 0.6 copy-done.9
  17.0 32.1 %reduce-scatter.2.cloned.1.call-done = f32[32,2,128]{2,0,1:T(8,128)} async-done(((f32[256,2,128]{2,0,1:T(8,128)}), f32[32,2,128]{2,0,1:T(8,128)}) %reduce-scatter.2.cloned.1.call-update) | async-done | bytes 32784 | tf_op jit(solution)/shard_map/reduce_scatter | solution.py:105
  49.1 1.0 %convolution_bitcast_fusion = f32[4,8,8]{2,1,0:T(8,128)S(1)} fusion(f32[128]{0:T(128)S(1)} %broadcast_multiply_fusion.3, f32[32,2,128]{2,0,1:T(8,128)} %reduce-scatter.2.cloned.1.call-done), kind=kOutput, calls=%fused_computation.14 | convolution fusion | flops 794624 | bytes 34304 | tf_op jit(solution)/shard_map/aicn,ajcn,n->aij/dot_general | solution.py:49
  50.2 9.9 %psum.7 = f32[4,64]{1,0:T(4,128)S(1)} all-reduce(f32[4,64]{1,0:T(4,128)S(1)} %reshape.79), channel_id=1, replica_groups=mesh['pw'=8,'band'=4] {'band'}, use_global_device_ids=true, to_apply=%region_2.0 | all-reduce | flops 256 | bytes 2048 | tf_op jit(solution)/shard_map/psum | solution.py:111
  60.1 0.4 fusion.31
  60.9 0.7 reshape.80
  61.8 14.0 %all_gather.3 = bf16[256,2,128]{2,0,1:T(8,128)(2,1)S(1)} all-gather(bf16[32,2,128]{2,0,1:T(8,128)(2,1)S(1)} %bitcast.79), channel_id=1, replica_groups=mesh['pw'=8,'band'=4] {'pw'}, dimensions={0}, use_global_device_ids=true | all-gather | bytes 147456 | tf_op jit(solution)/shard_map/all_gather | solution.py:117
  75.8 0.3 fusion.17
  76.1 0.3 fusion.16
  76.4 0.3 fusion.2
  76.8 0.3 fusion.3
  77.1 0.7 pad_maximum_fusion.1
  (41 shorter events, 3.0 us)
Async XLA Ops:
  7.2 52.9 %copy-start = (f32[4,64,64]{2,1,0:T(8,128)S(1)}, f32[4,64,64]{2,1,0:T(8,128)}, u32[]{:S(2)}) copy-start(f32[4,64,64]{2,1,0:T(8,128)} %param.18) | copy-start | bytes 196612
  7.2 42.0 %reduce-scatter.2.cloned.1.call-start = ((), (), s32[]{:S(2)}) async-start(), calls=%async_computation.1 | async-start | bytes 294912 | tf_op jit(solution)/shard_map/reduce_scatter | solution.py:105
  7.9 0.7 copy-start.1
  8.6 0.7 copy-start.8
  9.3 0.7 copy-start.4
  9.5 0.7 copy-start.6
  10.4 0.7 copy-start.7
  12.7 1.0 %copy-start.3 = (bf16[2,512,128]{2,1,0:T(8,128)(2,1)S(1)}, bf16[2,512,128]{2,1,0:T(8,128)(2,1)}, u32[]{:S(2)}) copy-start(bf16[2,512,128]{2,1,0:T(8,128)(2,1)} %param.10) | copy-start | bytes 786436
  15.5 0.7 copy-start.5
  16.3 0.7 copy-start.9
  60.8 0.8 copy-start.2
Sparse Core Ops, SparseCore 0:
  15.6 33.4 reduce-scatter.1
where the time goes:
time: 85.2 us; the launch traced here: 84.7 us
  waiting for transfers between devices  32.2 us (38%)
  blocking collectives  23.8 us (28%)
  between operations  14.2 us (17%)
  local copies, waits for them, and re-layouts  6.47 us (8%)
  matrix products  5.02 us (6%)
  other arithmetic  2.96 us (3%)
    reduce_scatter x1, waiting for transfers between devices, local(): lax.psum_scatter(project(beta_real, beta_imag, wave_real, wave_imag), 'pw...  32.1 us
    all_gather x1, blocking collectives, local(): lax.all_gather(weighted, 'pw', axis=0, tiled=True)  14 us
    psum x1, blocking collectives, local(): occupancy = lax.psum(occupancy_terms(projections, weights), 'band')  9.88 us
    unnamed x22, local copies, waits for them, and re-layouts  4.07 us
  transfers between devices with their start and end apart: 1, of which 1 were waited for; matrix products, arithmetic and copies ran while one was open for 0% of the time, Pallas kernels for 0%

commit v1 on v0

v1 whole, which is shorter than its diff:
```python
import functools
import math

import jax
import jax.numpy as jnp
import numpy as np
from jax import lax
from jax.experimental import pallas as pl
from jax.experimental.pallas import tpu as pltpu
from jax.sharding import PartitionSpec as P

MESH = pl.DeviceIdType.MESH
HIGH = lax.Precision.HIGHEST
BF = jnp.bfloat16
F32 = jnp.float32


def even_fit(function, degree):
    nodes = 0.125 + 0.125 * np.cos(np.pi * (np.arange(64) + 0.5) / 64)
    fit = np.polynomial.Chebyshev.fit(nodes, function(np.sqrt(nodes)), degree, domain=[0.0, 0.25])
    return [float(c) for c in fit.convert(kind=np.polynomial.Polynomial, domain=[-1, 1]).coef]


COS = even_fit(lambda t: np.cos(2 * np.pi * t), 7)
SIN = even_fit(lambda t: np.sin(2 * np.pi * t) / t, 7)


def series(coefs, u):
    value = jnp.full_like(u, coefs[-1])
    for c in coefs[-2::-1]:
        value = value * u + c
    return value


def iota(shape, dim):
    return lax.broadcasted_iota(jnp.int32, shape, dim)


def kernel(
    n,
    nb,
    wave,
    miller,
    reciprocal,
    fractional,
    species,
    order,
    widths,
    base,
    coupling,
    occ,
    applied,
    onsite,
    wv,
    xs,
    cs,
    sn,
    amp,
    beta,
    beta_t,
    part,
    rs_in,
    p_all,
    occ_out,
    occ_in,
    d_all,
    ww,
    load_sem,
    rs_s,
    rs_r,
    ag_s,
    ag_r,
    d_s,
    d_r,
    oc_s,
    oc_r,
):
    me = lax.axis_index("pw")
    mb = lax.axis_index("band")
    npw = wave.shape[1]
    bands = wave.shape[2]
    atoms = order.shape[0]
    own = atoms // n
    rows = own * 8
    every = atoms * 8

    barrier = pltpu.get_barrier_semaphore()
    for s in range(1, n):
        pl.semaphore_signal(
            barrier, inc=1, device_id={"pw": lax.rem(me + s, n)}, device_id_type=MESH
        )
    for s in range(1, nb):
        pl.semaphore_signal(
            barrier, inc=1, device_id={"band": lax.rem(mb + s, nb)}, device_id_type=MESH
        )

    loads = [
        pltpu.make_async_copy(wave.at[0], wv.at[pl.ds(0, npw), pl.ds(0, bands)], load_sem.at[0]),
        pltpu.make_async_copy(
            wave.at[1], wv.at[pl.ds(0, npw), pl.ds(bands, bands)], load_sem.at[1]
        ),
        pltpu.make_async_copy(wave.at[1], wv.at[pl.ds(npw, npw), pl.ds(0, bands)], load_sem.at[2]),
    ]
    for copy in loads:
        copy.start()

    m = [miller[c : c + 1, :].astype(F32) for c in range(3)]
    g = [
        (2.0 * math.pi)
        * (reciprocal[c, 0] * m[0] + reciprocal[c, 1] * m[1] + reciprocal[c, 2] * m[2])
        for c in range(3)
    ]
    g2 = g[0] * g[0] + g[1] * g[1] + g[2] * g[2]
    j = iota((8, npw), 0)
    is_s = j < 2
    wide = [jnp.broadcast_to(v, (8, npw)) for v in g]
    factor = jnp.where(
        (j == 2) | (j == 5), wide[0], jnp.where((j == 3) | (j == 6), wide[1], wide[2])
    )
    half = jnp.broadcast_to(-0.5 * g2, (8, npw))
    for s in range(widths.shape[0]):
        w = jnp.where(
            j == 0,
            widths[s, 0],
            jnp.where(j == 1, widths[s, 1], jnp.where(j < 5, widths[s, 2], widths[s, 3])),
        )
        amp[s] = jnp.where(is_s, 1.0, factor * w) * jnp.exp(half * (w * w))

    def position(k, carry):
        a = order[k]
        xs[pl.ds(k, 1), :] = (
            fractional[0, a] * m[0] + fractional[1, a] * m[1] + fractional[2, a] * m[2]
        )
        return carry

    lax.fori_loop(0, atoms, position, 0, unroll=8)
    x = xs[...]
    t = x - jnp.round(x)
    u = t * t
    cs[...] = series(COS, u)
    sn[...] = t * series(SIN, u)

    def projector(pair, carry):
        real, imag = [], []
        for e in range(2):
            k = pair * 2 + e
            c = jnp.broadcast_to(cs[pl.ds(k, 1), :], (8, npw))
            s = jnp.broadcast_to(sn[pl.ds(k, 1), :], (8, npw))
            a = amp[species[order[k]]]
            real.append(a * jnp.where(is_s, c, -s))
            imag.append(-a * jnp.where(is_s, s, c))
        at = pl.ds(pl.multiple_of(pair * 16, 16), 16)
        beta[at, 0:npw] = jnp.concatenate(real, axis=0).astype(BF)
        beta[at, npw : 2 * npw] = jnp.concatenate(imag, axis=0).astype(BF)
        return carry

    lax.fori_loop(0, atoms // 2, projector, 0, unroll=4)

    for copy in loads:
        copy.wait()
    wv[npw : 2 * npw, bands : 2 * bands] = -wv[0:npw, 0:bands]
    part[...] = jnp.dot(beta[...], wv[...], preferred_element_type=F32).astype(BF)
    pl.semaphore_wait(barrier, n - 1 + nb - 1)

    def block(index):
        return pl.ds(pl.multiple_of(index * rows, rows), rows)

    sends = []
    for s in range(1, n):
        to = lax.rem(me + s, n)
        copy = pltpu.make_async_remote_copy(
            src_ref=part.at[block(to)],
            dst_ref=rs_in.at[s],
            send_sem=rs_s.at[s],
            recv_sem=rs_r.at[s],
            device_id={"pw": to},
            device_id_type=MESH,
        )
        copy.start()
        sends.append(copy)

    beta_t[:, 0:every] = beta[:, 0:npw].T
    beta_t[:, every : 2 * every] = beta[:, npw : 2 * npw].T
    weights = occ[...] * (1.0 / (bands * nb))
    weights = jnp.concatenate([weights, weights], axis=1)
    kinds = [species[order[me * own + k]] for k in range(own)]
    base8 = jnp.concatenate([base[kind] for kind in kinds], axis=1)
    spread = (
        (iota((rows, own * 64), 0) // 8 == iota((rows, own * 64), 1) // 64)
        & (iota((rows, own * 64), 0) % 8 == iota((rows, own * 64), 1) % 8)
    ).astype(F32)
    gather = (
        (iota((own * 64, rows), 1) // 8 == iota((own * 64, rows), 0) // 64)
        & (iota((own * 64, rows), 1) % 8 == iota((own * 64, rows), 0) % 8)
    ).astype(F32)
    row_of = (iota((8, own * 64), 1) % 64) // 8 == iota((8, own * 64), 0)
    diagonal = iota((rows, rows), 0) // 8 == iota((rows, rows), 1) // 8

    total = part[block(me), :].astype(F32)
    for s in range(1, n):
        sends[s - 1].wait_recv()
        total = total + rs_in[s].astype(F32)
    p_all[0] = total.astype(BF)
    gram = lax.dot_general(
        total * weights, total, (((1,), (1,)), ((), ())), precision=HIGH, preferred_element_type=F32
    )
    gram = jnp.where(diagonal, gram, 0.0)
    occ8 = gram[0:8, :]
    for k in range(1, own):
        occ8 = occ8 + gram[k * 8 : k * 8 + 8, :]
    occ_out[:, 0:rows] = occ8

    occ_sends = []
    for s in range(1, nb):
        copy = pltpu.make_async_remote_copy(
            src_ref=occ_out,
            dst_ref=occ_in.at[s],
            send_sem=oc_s.at[s],
            recv_sem=oc_r.at[s],
            device_id={"band": lax.rem(mb + s, nb)},
            device_id_type=MESH,
        )
        copy.start()
        occ_sends.append(copy)
    p_sends = []
    for s in range(1, n):
        copy = pltpu.make_async_remote_copy(
            src_ref=p_all.at[0],
            dst_ref=p_all.at[s],
            send_sem=ag_s.at[s],
            recv_sem=ag_r.at[s],
            device_id={"pw": lax.rem(me + s, n)},
            device_id_type=MESH,
        )
        copy.start()
        p_sends.append(copy)

    for copy in occ_sends:
        copy.wait_recv()
    occ_in[0] = occ_out[...]
    occ8 = occ_in[lax.rem(mb + nb, nb)][:, 0:rows]
    for b in range(1, nb):
        occ8 = occ8 + occ_in[lax.rem(mb - b + nb, nb)][:, 0:rows]
    flat = jnp.dot(occ8, spread, precision=HIGH, preferred_element_type=F32)
    flat = jnp.sum(jnp.where(row_of, flat, 0.0), axis=0, keepdims=True)
    answers = []
    for k in range(own):
        line = jnp.broadcast_to(flat[:, k * 64 : k * 64 + 64], (8, 64))
        answers.append(
            lax.dot_general(
                line,
                coupling[kinds[k]],
                (((1,), (1,)), ((), ())),
                precision=HIGH,
                preferred_element_type=F32,
            )
        )
    answer = jnp.where(row_of, jnp.concatenate(answers, axis=1), 0.0)
    d8 = base8 + jnp.dot(answer, gather, precision=HIGH, preferred_element_type=F32)
    d_all[0, :, 0:rows] = d8

    d_sends = []
    for s in range(1, n):
        copy = pltpu.make_async_remote_copy(
            src_ref=d_all.at[0],
            dst_ref=d_all.at[s],
            send_sem=d_s.at[s],
            recv_sem=d_r.at[s],
            device_id={"pw": lax.rem(me + s, n)},
            device_id_type=MESH,
        )
        copy.start()
        d_sends.append(copy)
    for k in range(own):
        onsite[k] = d8[:, k * 8 : k * 8 + 8]

    for s in range(n):
        if s:
            p_sends[s - 1].wait_recv()
            d_sends[s - 1].wait_recv()
        mine = d_all[s][:, 0:rows]
        square = jnp.where(diagonal, jnp.concatenate([mine] * own, axis=0), 0.0)
        upper = square.astype(BF)
        lower = (square - upper.astype(F32)).astype(BF)
        p = p_all[s]
        w = jnp.dot(upper, p, preferred_element_type=F32) + jnp.dot(
            lower, p, preferred_element_type=F32
        )
        w = w.astype(BF)
        owner = lax.rem(me - s + n, n)
        ww[block(owner), :] = w
        second = pl.ds(pl.multiple_of(every + owner * rows, rows), rows)
        ww[second, 0:bands] = -w[:, bands : 2 * bands]
        ww[second, bands : 2 * bands] = w[:, 0:bands]
    result = jnp.dot(beta_t[...], ww[...], preferred_element_type=F32).astype(BF)
    applied[0] = result[:, 0:bands]
    applied[1] = result[:, bands : 2 * bands]
    for copy in sends + occ_sends + p_sends + d_sends:
        copy.wait_send()


def solution(mesh):
    n, nb = mesh.shape["pw"], mesh.shape["band"]

    def local(wave, miller, reciprocal, fractional, species, order, widths, base, coupling, occ):
        _, npw, bands = wave.shape
        atoms = order.shape[0]
        own = atoms // n
        rows, every = own * 8, atoms * 8
        lanes = -(-rows // 128) * 128
        vmem = pl.BlockSpec(memory_space=pltpu.VMEM)
        smem = pl.BlockSpec(memory_space=pltpu.SMEM)
        dma = pltpu.SemaphoreType.DMA
        return pl.pallas_call(
            functools.partial(kernel, n, nb),
            out_shape=(
                jax.ShapeDtypeStruct(wave.shape, BF),
                jax.ShapeDtypeStruct((own, 8, 8), F32),
            ),
            in_specs=[
                pl.BlockSpec(memory_space=pl.ANY),
                vmem,
                smem,
                smem,
                smem,
                smem,
                smem,
                vmem,
                vmem,
                vmem,
            ],
            out_specs=(vmem, vmem),
            scratch_shapes=[
                pltpu.VMEM((2 * npw, 2 * bands), BF),
                pltpu.VMEM((atoms, npw), F32),
                pltpu.VMEM((atoms, npw), F32),
                pltpu.VMEM((atoms, npw), F32),
                pltpu.VMEM((widths.shape[0], 8, npw), F32),
                pltpu.VMEM((every, 2 * npw), BF),
                pltpu.VMEM((npw, 2 * every), BF),
                pltpu.VMEM((every, 2 * bands), BF),
                pltpu.VMEM((n, rows, 2 * bands), BF),
                pltpu.VMEM((n, rows, 2 * bands), BF),
                pltpu.VMEM((8, lanes), F32),
                pltpu.VMEM((nb, 8, lanes), F32),
                pltpu.VMEM((n, 8, lanes), F32),
                pltpu.VMEM((2 * every, 2 * bands), BF),
                dma((3,)),
                dma((n,)),
                dma((n,)),
                dma((n,)),
                dma((n,)),
                dma((n,)),
                dma((n,)),
                dma((nb,)),
                dma((nb,)),
            ],
            compiler_params=pltpu.CompilerParams(collective_id=0, has_side_effects=True),
        )(
            wave,
            miller,
            reciprocal,
            fractional,
            species,
            order,
            widths,
            base,
            coupling,
            occ.reshape(1, bands),
        )

    placed = (P(None, "pw", "band"), P(None, "pw"), P(), P(), P(), P(), P(), P(), P(), P("band"))
    return jax.shard_map(
        local,
        mesh=mesh,
        in_specs=placed,
        out_specs=(P(None, "pw", "band"), P("pw", None, None)),
        check_vma=False,
    )
```

time: 85.2 us -> 24.8 us (0.29)
  waiting for transfers between devices: 32.2 us -> 0 us
  blocking collectives: 23.8 us -> 0 us
  Pallas kernels: 0 us -> 21.7 us
  between operations: 14.2 us -> 0.65 us
  matrix products: 5.02 us -> 0 us
  local copies, waits for them, and re-layouts: 6.47 us -> 2.28 us
  other arithmetic: 2.96 us -> 0 us
    reduce_scatter x1 -> x0, waiting for transfers between devices: 32.1 us -> none  [local(): lax.psum_scatter(project(beta_real, beta_imag, wave_real, wave_imag), 'pw...]
    pallas_call x0 -> x1, Pallas kernels: none -> 21.7 us  [local(): pl.pallas_call(functools.partial(kernel, n, nb), out_shape=(jax.ShapeDtyp...]
    all_gather x1 -> x0, blocking collectives: 14 us -> none  [local(): lax.all_gather(weighted, 'pw', axis=0, tiled=True)]
    psum x1 -> x0, blocking collectives: 9.88 us -> none  [local(): occupancy = lax.psum(occupancy_terms(projections, weights), 'band')]
    dot_general x16 -> x0, matrix products: 5.02 us -> none  [the longest x1 0.98 us: occupancy_terms(): jnp.einsum('aicn,ajcn,n->aij', grouped, grouped, weights, precision=HIGH)]
    unnamed x22 -> x4, local copies, waits for them, and re-layouts: 4.07 us -> 2.28 us
    another operation x4 -> x0, other arithmetic: 1.78 us -> none  [the longest x1 0.73 us: back_project(): return jnp.stack([out_real, out_imag], axis=0)]
    gather x2 -> x0, local copies, waits for them, and re-layouts: 1.27 us -> none  [the longest x1 0.7 us: local(): sorted_species = species[atom_order]]
  transfers between devices with their start and end apart: 1 -> 0, of which waited for: 1 -> 0; matrix products, arithmetic and copies ran while one was open for 0% -> 0% of each run, Pallas kernels for 0% -> 0%
where the time goes in v1:
time: 24.8 us; the launch traced here: 24.7 us
  Pallas kernels  21.7 us (88%)
  local copies, waits for them, and re-layouts  2.28 us (9%)
  between operations  0.65 us (3%)
    pallas_call x1, Pallas kernels, local(): pl.pallas_call(functools.partial(kernel, n, nb), out_shape=(jax.ShapeDtyp...  21.7 us
    unnamed x4, local copies, waits for them, and re-layouts  2.28 us

profile of v1, /device:TPU:0, one launch (start us, length us, event | category | flops | bytes accessed | tf_op | source)
XLA Modules:
  0.0 24.7 jit_solution(8443106451961298079)
XLA Ops:
  0.6 21.7 %shard_map.113 = (bf16[2,512,128]{2,1,0:T(8,128)(2,1)}, f32[4,8,8]{2,1,0:T(8,128)}) custom-call(bf16[2,512,128]{2,1,0:T(8,128)(2,1)} %wave.1, s32[3,512]{1,0:T(4,128)} %miller.1, f32[3,3]{1,0:T(4,128)} %reciprocal.1, f32[3,32]{1,0:T(4,128)} %fractional.1, s32[32]{0:T(128)} %species.1, s32[32]{0:T(128)} %order.1, f32[4,4]{1,0:T(4,128)} %widths.1, ...), custom_call_target="tpu_custom_call" | custom-call | tf_op jit(solution)/shard_map/pallas_call | solution.py:314
  22.4 0.0 copy-start
  22.4 1.7 %copy.14 = bf16[2,512,128]{2,1,0:T(8,128)(2,1)} copy(bf16[2,512,128]{2,1,0:T(8,128)(2,1)} %get-tuple-element.4) | data formatting | bytes 524288
  24.1 0.0 copy-done
  24.1 0.6 %copy.15 = f32[4,8,8]{2,1,0:T(8,128)} copy(f32[4,8,8]{2,1,0:T(8,128)S(1)} %copy-done) | data formatting | bytes 2048
Async XLA Ops:
  22.4 1.7 %copy-start = (f32[4,8,8]{2,1,0:T(8,128)S(1)}, f32[4,8,8]{2,1,0:T(8,128)}, u32[]{:S(2)}) copy-start(f32[4,8,8]{2,1,0:T(8,128)} %get-tuple-element.5) | copy-start | bytes 3076

commit v2 on v1

v2 whole, which is shorter than its diff:
```python
import functools
import math

import jax
import jax.numpy as jnp
import numpy as np
from jax import lax
from jax.experimental import pallas as pl
from jax.experimental.pallas import tpu as pltpu
from jax.sharding import PartitionSpec as P

MESH = pl.DeviceIdType.MESH
HIGH = lax.Precision.HIGHEST
BF = jnp.bfloat16
F32 = jnp.float32


def even_fit(function, degree):
    nodes = 0.125 + 0.125 * np.cos(np.pi * (np.arange(64) + 0.5) / 64)
    fit = np.polynomial.Chebyshev.fit(nodes, function(np.sqrt(nodes)), degree, domain=[0.0, 0.25])
    return [float(c) for c in fit.convert(kind=np.polynomial.Polynomial, domain=[-1, 1]).coef]


COS = even_fit(lambda t: np.cos(2 * np.pi * t), 7)
SIN = even_fit(lambda t: np.sin(2 * np.pi * t) / t, 7)


def series(coefs, u):
    value = jnp.full_like(u, coefs[-1])
    for c in coefs[-2::-1]:
        value = value * u + c
    return value


def iota(shape, dim):
    return lax.broadcasted_iota(jnp.int32, shape, dim)


def kernel(
    n,
    nb,
    wave,
    miller_h,
    reciprocal_h,
    fractional_h,
    species_h,
    order_h,
    widths_h,
    base_h,
    coupling_h,
    occ_h,
    applied,
    onsite,
    miller,
    reciprocal,
    fractional,
    species,
    order,
    widths,
    base,
    coupling,
    occ,
    wv,
    xs,
    cs,
    sn,
    amp,
    beta,
    beta_t,
    part,
    rs_in,
    p_all,
    o_in,
    o_sum,
    respond,
    ww,
    load_sem,
    rs_s,
    rs_r,
    ag_s,
    ag_r,
    oc_s,
    oc_r,
):
    me = lax.axis_index("pw")
    mb = lax.axis_index("band")
    npw = wave.shape[1]
    bands = wave.shape[2]
    atoms = order.shape[0]
    kinds = widths.shape[0]
    own = atoms // n
    pack = own // 2
    rows = own * 8
    every = atoms * 8
    peers = n * nb

    small = [
        (miller_h, miller),
        (reciprocal_h, reciprocal),
        (fractional_h, fractional),
        (species_h, species),
        (order_h, order),
        (widths_h, widths),
        (base_h, base),
        (coupling_h, coupling),
        (occ_h, occ),
        (wave.at[0], wv.at[pl.ds(0, npw), pl.ds(0, bands)]),
        (wave.at[1], wv.at[pl.ds(0, npw), pl.ds(bands, bands)]),
        (wave.at[1], wv.at[pl.ds(npw, npw), pl.ds(0, bands)]),
    ]
    loads = [
        pltpu.make_async_copy(source, to, load_sem.at[i]) for i, (source, to) in enumerate(small)
    ]
    for copy in loads:
        copy.start()
    barrier = pltpu.get_barrier_semaphore()

    def place(q):
        return {"pw": lax.rem(me + q // nb, n), "band": lax.rem(mb + lax.rem(q, nb), nb)}

    def greet(q, carry):
        pl.semaphore_signal(barrier, inc=1, device_id=place(q), device_id_type=MESH)
        return carry

    lax.fori_loop(1, peers, greet, 0)
    for copy in loads[0:6]:
        copy.wait()

    m = [miller[c : c + 1, :].astype(F32) for c in range(3)]
    g = [
        (2.0 * math.pi)
        * (reciprocal[c, 0] * m[0] + reciprocal[c, 1] * m[1] + reciprocal[c, 2] * m[2])
        for c in range(3)
    ]
    g2 = g[0] * g[0] + g[1] * g[1] + g[2] * g[2]
    j = iota((8, npw), 0)
    is_s = j < 2
    wide = [jnp.broadcast_to(v, (8, npw)) for v in g]
    factor = jnp.where(
        (j == 2) | (j == 5), wide[0], jnp.where((j == 3) | (j == 6), wide[1], wide[2])
    )
    half = jnp.broadcast_to(-0.5 * g2, (8, npw))
    for s in range(widths.shape[0]):
        w = jnp.where(
            j == 0,
            widths[s, 0],
            jnp.where(j == 1, widths[s, 1], jnp.where(j < 5, widths[s, 2], widths[s, 3])),
        )
        amp[s] = jnp.where(is_s, 1.0, factor * w) * jnp.exp(half * (w * w))

    def position(k, carry):
        a = order[k]
        xs[pl.ds(k, 1), :] = (
            fractional[0, a] * m[0] + fractional[1, a] * m[1] + fractional[2, a] * m[2]
        )
        return carry

    lax.fori_loop(0, atoms, position, 0, unroll=8)
    x = xs[...]
    t = x - jnp.round(x)
    u = t * t
    cs[...] = series(COS, u)
    sn[...] = t * series(SIN, u)

    def projector(pair, carry):
        real, imag = [], []
        for e in range(2):
            k = pair * 2 + e
            c = jnp.broadcast_to(cs[pl.ds(k, 1), :], (8, npw))
            s = jnp.broadcast_to(sn[pl.ds(k, 1), :], (8, npw))
            a = amp[species[order[k]]]
            real.append(a * jnp.where(is_s, c, -s))
            imag.append(-a * jnp.where(is_s, s, c))
        at = pl.ds(pl.multiple_of(pair * 16, 16), 16)
        beta[at, 0:npw] = jnp.concatenate(real, axis=0).astype(BF)
        beta[at, npw : 2 * npw] = jnp.concatenate(imag, axis=0).astype(BF)
        return carry

    lax.fori_loop(0, atoms // 2, projector, 0, unroll=4)

    for copy in loads[6:]:
        copy.wait()
    wv[npw : 2 * npw, bands : 2 * bands] = -wv[0:npw, 0:bands]
    part[...] = jnp.dot(beta[...], wv[...], preferred_element_type=F32).astype(BF)
    pl.semaphore_wait(barrier, peers - 1)

    def block(index):
        return pl.ds(pl.multiple_of(index * rows, rows), rows)

    sends = []
    for s in range(1, n):
        to = lax.rem(me + s, n)
        copy = pltpu.make_async_remote_copy(
            src_ref=part.at[block(to)],
            dst_ref=rs_in.at[s],
            send_sem=rs_s.at[s],
            recv_sem=rs_r.at[s],
            device_id={"pw": to},
            device_id_type=MESH,
        )
        copy.start()
        sends.append(copy)

    beta_t[:, 0:every] = beta[:, 0:npw].T
    beta_t[:, every : 2 * every] = beta[:, npw : 2 * npw].T
    weights = occ[...] * (1.0 / (bands * nb))
    weights = jnp.concatenate([weights, weights], axis=1)
    spread = (
        (iota((rows, own * 64), 0) // 8 == iota((rows, own * 64), 1) // 64)
        & (iota((rows, own * 64), 0) % 8 == iota((rows, own * 64), 1) % 8)
    ).astype(F32)
    row_of = (iota((8, own * 64), 1) % 64) // 8 == iota((8, own * 64), 0)
    diagonal = iota((rows, rows), 0) // 8 == iota((rows, rows), 1) // 8
    gather = (iota((128, rows), 0) % 8 == iota((128, rows), 1) % 8).astype(BF)
    flipped = coupling[...].reshape(kinds * 64, 64).T
    upper = flipped.astype(BF)
    lower = (flipped - upper.astype(F32)).astype(BF)
    none = jnp.zeros_like(upper)
    for i, piece in enumerate((upper, upper, lower)):
        respond[i * 128 : i * 128 + 64, :] = jnp.concatenate([piece, none], axis=1)
        respond[i * 128 + 64 : i * 128 + 128, :] = jnp.concatenate([none, piece], axis=1)
    line = iota((n * pack, 64), 0)
    kind_of = []
    for parity in range(2):
        column = jnp.zeros((n * pack, 64), jnp.int32)
        for row in range(n * pack):
            owner = lax.rem(me - row // pack + n, n)
            kind = species[order[owner * own + (row % pack) * 2 + parity]]
            column = jnp.where(line == row, kind, column)
        kind_of.append(column)
    fan = (iota((8, 64), 1) % 8 == iota((8, 64), 0)).astype(F32)
    mine = iota((8, 64), 1) // 8 == iota((8, 64), 0)
    bare = [jnp.zeros((n * pack, 64), F32)] * 2
    for kind in range(kinds):
        flat = jnp.dot(base[kind], fan, precision=HIGH, preferred_element_type=F32)
        flat = jnp.sum(jnp.where(mine, flat, 0.0), axis=0, keepdims=True)
        for parity in range(2):
            bare[parity] = jnp.where(kind_of[parity] == kind, flat, bare[parity])
    member = iota((8, 128), 0) == (iota((8, 128), 1) % 64) // 8
    picks = [member & (iota((8, 128), 1) // 64 == parity) for parity in range(2)]

    total = part[block(me), :].astype(F32)
    for s in range(1, n):
        sends[s - 1].wait_recv()
        total = total + rs_in[s].astype(F32)
    p_all[0] = total.astype(BF)
    gram = lax.dot_general(
        total * weights, total, (((1,), (1,)), ((), ())), precision=HIGH, preferred_element_type=F32
    )
    gram = jnp.where(diagonal, gram, 0.0)
    occ8 = gram[0:8, :]
    for k in range(1, own):
        occ8 = occ8 + gram[k * 8 : k * 8 + 8, :]
    flat = jnp.dot(occ8, spread, precision=HIGH, preferred_element_type=F32)
    flat = jnp.sum(jnp.where(row_of, flat, 0.0), axis=0, keepdims=True)
    for r in range(pack):
        o_in[0, r : r + 1, :] = flat[:, r * 128 : r * 128 + 128]

    def occupancy_copy(q):
        return pltpu.make_async_remote_copy(
            src_ref=o_in.at[0],
            dst_ref=o_in.at[q],
            send_sem=oc_s.at[q],
            recv_sem=oc_r.at[q],
            device_id=place(q),
            device_id_type=MESH,
        )

    def tell(q, carry):
        occupancy_copy(q).start()
        return carry

    lax.fori_loop(1, peers, tell, 0)
    p_sends = []
    for s in range(1, n):
        copy = pltpu.make_async_remote_copy(
            src_ref=p_all.at[0],
            dst_ref=p_all.at[s],
            send_sem=ag_s.at[s],
            recv_sem=ag_r.at[s],
            device_id={"pw": lax.rem(me + s, n)},
            device_id_type=MESH,
        )
        copy.start()
        p_sends.append(copy)

    def hear(q, carry):
        occupancy_copy(q).wait_recv()
        return carry

    lax.fori_loop(1, peers, hear, 0)
    for d in range(n):
        summed = o_in[d * nb + lax.rem(mb + nb, nb)]
        for b in range(1, nb):
            summed = summed + o_in[d * nb + lax.rem(mb - b + nb, nb)]
        o_sum[d * pack : d * pack + pack, :] = summed
    summed = o_sum[...]
    upper = summed.astype(BF)
    lower = (summed - upper.astype(F32)).astype(BF)
    answer = jnp.dot(
        jnp.concatenate([upper, lower, upper], axis=1), respond[...], preferred_element_type=F32
    )
    matrix = []
    for parity in range(2):
        chosen = jnp.zeros((n * pack, 64), F32)
        for kind in range(kinds):
            at = (parity * kinds + kind) * 64
            chosen = jnp.where(kind_of[parity] == kind, answer[:, at : at + 64], chosen)
        matrix.append(bare[parity] + chosen)
    matrix = jnp.concatenate(matrix, axis=1)
    o_sum[...] = matrix

    for s in range(n):
        lines = []
        for k in range(own):
            at = s * pack + k // 2
            lines.append(
                jnp.where(picks[k % 2], jnp.broadcast_to(o_sum[at : at + 1, :], (8, 128)), 0.0)
            )
        lines = jnp.concatenate(lines, axis=0)
        upper = lines.astype(BF)
        lower = (lines - upper.astype(F32)).astype(BF)
        square = jnp.dot(
            jnp.concatenate([upper, lower], axis=0), gather, preferred_element_type=F32
        )
        upper = jnp.where(diagonal, square[0:rows, :], 0.0)
        lower = jnp.where(diagonal, square[rows : 2 * rows, :], 0.0)
        if s == 0:
            both = upper + lower
            for k in range(own):
                onsite[k] = both[k * 8 : k * 8 + 8, k * 8 : k * 8 + 8]
        if s:
            p_sends[s - 1].wait_recv()
        p = p_all[s]
        w = jnp.dot(
            jnp.concatenate([upper, lower], axis=0).astype(BF), p, preferred_element_type=F32
        )
        w = (w[0:rows, :] + w[rows : 2 * rows, :]).astype(BF)
        owner = lax.rem(me - s + n, n)
        ww[block(owner), :] = w
        second = pl.ds(pl.multiple_of(every + owner * rows, rows), rows)
        ww[second, 0:bands] = -w[:, bands : 2 * bands]
        ww[second, bands : 2 * bands] = w[:, 0:bands]
    result = jnp.dot(beta_t[...], ww[...], preferred_element_type=F32).astype(BF)
    applied[0] = result[:, 0:bands]
    applied[1] = result[:, bands : 2 * bands]
    for copy in sends + p_sends:
        copy.wait_send()

    def told(q, carry):
        occupancy_copy(q).wait_send()
        return carry

    lax.fori_loop(1, peers, told, 0)


def finish(applied_in, onsite_in, applied, onsite, sem):
    copies = [
        pltpu.make_async_copy(applied_in, applied, sem.at[0]),
        pltpu.make_async_copy(onsite_in, onsite, sem.at[1]),
    ]
    for copy in copies:
        copy.start()
    for copy in copies:
        copy.wait()


def solution(mesh):
    n, nb = mesh.shape["pw"], mesh.shape["band"]

    def local(wave, miller, reciprocal, fractional, species, order, widths, base, coupling, occ):
        _, npw, bands = wave.shape
        atoms = order.shape[0]
        own = atoms // n
        rows, every = own * 8, atoms * 8
        pack = own // 2
        kinds = widths.shape[0]
        vmem = pl.BlockSpec(memory_space=pltpu.VMEM)
        hbm = pl.BlockSpec(memory_space=pltpu.HBM)
        dma = pltpu.SemaphoreType.DMA
        results = (
            jax.ShapeDtypeStruct(wave.shape, BF),
            jax.ShapeDtypeStruct((own, 8, 8), F32),
        )
        first = pl.pallas_call(
            functools.partial(kernel, n, nb),
            out_shape=results,
            in_specs=[hbm] * 10,
            out_specs=(vmem, vmem),
            scratch_shapes=[
                pltpu.VMEM(miller.shape, jnp.int32),
                pltpu.SMEM(reciprocal.shape, F32),
                pltpu.SMEM(fractional.shape, F32),
                pltpu.SMEM(species.shape, jnp.int32),
                pltpu.SMEM(order.shape, jnp.int32),
                pltpu.SMEM(widths.shape, F32),
                pltpu.VMEM(base.shape, F32),
                pltpu.VMEM(coupling.shape, F32),
                pltpu.VMEM((1, bands), F32),
                pltpu.VMEM((2 * npw, 2 * bands), BF),
                pltpu.VMEM((atoms, npw), F32),
                pltpu.VMEM((atoms, npw), F32),
                pltpu.VMEM((atoms, npw), F32),
                pltpu.VMEM((kinds, 8, npw), F32),
                pltpu.VMEM((every, 2 * npw), BF),
                pltpu.VMEM((npw, 2 * every), BF),
                pltpu.VMEM((every, 2 * bands), BF),
                pltpu.VMEM((n, rows, 2 * bands), BF),
                pltpu.VMEM((n, rows, 2 * bands), BF),
                pltpu.VMEM((n * nb, pack, 128), F32),
                pltpu.VMEM((n * pack, 128), F32),
                pltpu.VMEM((384, kinds * 128), BF),
                pltpu.VMEM((2 * every, 2 * bands), BF),
                dma((12,)),
                dma((n,)),
                dma((n,)),
                dma((n,)),
                dma((n,)),
                dma((n * nb,)),
                dma((n * nb,)),
            ],
            compiler_params=pltpu.CompilerParams(
                collective_id=0, has_side_effects=True, vmem_limit_bytes=40 * 2**20
            ),
        )(
            *[
                pltpu.with_memory_space_constraint(value, pltpu.HBM)
                for value in (
                    wave,
                    miller,
                    reciprocal,
                    fractional,
                    species,
                    order,
                    widths,
                    base,
                    coupling,
                    occ.reshape(1, bands),
                )
            ]
        )
        anywhere = pl.BlockSpec(memory_space=pl.ANY)
        return pl.pallas_call(
            finish,
            out_shape=results,
            in_specs=[anywhere] * 2,
            out_specs=(hbm, hbm),
            scratch_shapes=[dma((2,))],
            compiler_params=pltpu.CompilerParams(vmem_limit_bytes=2**20),
        )(*first)

    placed = (P(None, "pw", "band"), P(None, "pw"), P(), P(), P(), P(), P(), P(), P(), P("band"))
    return jax.shard_map(
        local,
        mesh=mesh,
        in_specs=placed,
        out_specs=(P(None, "pw", "band"), P("pw", None, None)),
        check_vma=False,
    )
```

time: 24.8 us -> 21 us (0.85)
  local copies, waits for them, and re-layouts: 2.28 us -> 0 us
  Pallas kernels: 21.7 us -> 20.2 us
    unnamed x4 -> x0, local copies, waits for them, and re-layouts: 2.28 us -> none
    pallas_call x1 -> x2, Pallas kernels: 21.7 us -> 20.2 us  [the longest x1 19.4 us: local(): pl.pallas_call(functools.partial(kernel, n, nb), out_shape=results, in_sp...]
where the time goes in v2:
time: 21 us; the launch traced here: 20.8 us
  Pallas kernels  20.2 us (96%)
  between operations  0.64 us (3%)
    pallas_call x1, Pallas kernels, local(): pl.pallas_call(functools.partial(kernel, n, nb), out_shape=results, in_sp...  19.4 us
    pallas_call x1, Pallas kernels, local(): pl.pallas_call(finish, out_shape=results, in_specs=[anywhere] * 2, out_sp...  0.72 us

profile of v2, /device:TPU:0, one launch (start us, length us, event | category | flops | bytes accessed | tf_op | source)
XLA Modules:
  0.0 20.8 jit_solution(8695479156228182278)
XLA Ops:
  0.6 19.4 %shard_map.113 = (bf16[2,512,128]{2,1,0:T(8,128)(2,1)S(1)}, f32[4,8,8]{2,1,0:T(8,128)S(1)}) custom-call(bf16[2,512,128]{2,1,0:T(8,128)(2,1)} %wave.1, s32[3,512]{1,0:T(4,128)} %miller_h.1, f32[3,3]{1,0:T(4,128)} %reciprocal_h.1, f32[3,32]{1,0:T(4,128)} %fractional_h.1, s32[32]{0:T(128)} %species_h.1, s32[32]{0:T(128)} %order_h.1, f32[4,4]{1,0:T(4,128)} %widths_h.1, ...), custom_call_target="tpu_custom_call" | custom-call | tf_op jit(solution)/shard_map/pallas_call | solution.py:385
  20.1 0.7 %shard_map.114 = (bf16[2,512,128]{2,1,0:T(8,128)(2,1)}, f32[4,8,8]{2,1,0:T(8,128)}) custom-call(bf16[2,512,128]{2,1,0:T(8,128)(2,1)S(1)} %get-tuple-element.4.applied_in, f32[4,8,8]{2,1,0:T(8,128)S(1)} %get-tuple-element.5.onsite_in), custom_call_target="tpu_custom_call" | custom-call | tf_op jit(solution)/shard_map/pallas_call | solution.py:443

commit v3 on v2

--- a/solution.py
+++ b/solution.py
@@ -81,6 +81,7 @@
     ag_r,
     oc_s,
     oc_r,
+    ready,
 ):
     me = lax.axis_index("pw")
     mb = lax.axis_index("band")
@@ -118,11 +119,21 @@
     def place(q):
         return {"pw": lax.rem(me + q // nb, n), "band": lax.rem(mb + lax.rem(q, nb), nb)}
 
-    def greet(q, carry):
-        pl.semaphore_signal(barrier, inc=1, device_id=place(q), device_id_type=MESH)
-        return carry
-
-    lax.fori_loop(1, peers, greet, 0)
+    def each(step):
+        if peers <= 64:
+            for q in range(1, peers):
+                step(q)
+        else:
+            lax.fori_loop(1, peers, lambda q, carry: (step(q), carry)[1], 0)
+
+    for d in range(1, n):
+        pl.semaphore_signal(
+            barrier, inc=1, device_id={"pw": lax.rem(me + d, n)}, device_id_type=MESH
+        )
+    for b in range(1, nb):
+        pl.semaphore_signal(
+            barrier, inc=1, device_id={"band": lax.rem(mb + b, nb)}, device_id_type=MESH
+        )
     for copy in loads[0:6]:
         copy.wait()
 
@@ -182,15 +193,14 @@
         copy.wait()
     wv[npw : 2 * npw, bands : 2 * bands] = -wv[0:npw, 0:bands]
     part[...] = jnp.dot(beta[...], wv[...], preferred_element_type=F32).astype(BF)
-    pl.semaphore_wait(barrier, peers - 1)
+    pl.semaphore_wait(barrier, n - 1 + nb - 1)
 
     def block(index):
         return pl.ds(pl.multiple_of(index * rows, rows), rows)
 
-    sends = []
-    for s in range(1, n):
+    def scatter(s):
         to = lax.rem(me + s, n)
-        copy = pltpu.make_async_remote_copy(
+        return pltpu.make_async_remote_copy(
             src_ref=part.at[block(to)],
             dst_ref=rs_in.at[s],
             send_sem=rs_s.at[s],
@@ -198,8 +208,19 @@
             device_id={"pw": to},
             device_id_type=MESH,
         )
-        copy.start()
-        sends.append(copy)
+
+    upper_half = me // (n // 2)
+    far_first = [
+        lax.rem(n - 2 - me + upper_half + (2 * upper_half - 1) * i + 2 * (n - 1), n - 1) + 1
+        for i in range(n - 1)
+    ]
+    sends = [scatter(s) for s in range(1, n)]
+    for s in far_first:
+        scatter(s).start()
+    for b in range(1, nb):
+        pl.semaphore_signal(
+            ready, inc=1, device_id={"band": lax.rem(mb + b, nb)}, device_id_type=MESH
+        )
 
     beta_t[:, 0:every] = beta[:, 0:npw].T
     beta_t[:, every : 2 * every] = beta[:, npw : 2 * npw].T
@@ -239,6 +260,7 @@
     member = iota((8, 128), 0) == (iota((8, 128), 1) % 64) // 8
     picks = [member & (iota((8, 128), 1) // 64 == parity) for parity in range(2)]
 
+    pl.semaphore_wait(ready, nb - 1)
     total = part[block(me), :].astype(F32)
     for s in range(1, n):
         sends[s - 1].wait_recv()
@@ -266,11 +288,7 @@
             device_id_type=MESH,
         )
 
-    def tell(q, carry):
-        occupancy_copy(q).start()
-        return carry
-
-    lax.fori_loop(1, peers, tell, 0)
+    each(lambda q: occupancy_copy(q).start())
     p_sends = []
     for s in range(1, n):
         copy = pltpu.make_async_remote_copy(
@@ -284,11 +302,7 @@
         copy.start()
         p_sends.append(copy)
 
-    def hear(q, carry):
-        occupancy_copy(q).wait_recv()
-        return carry
-
-    lax.fori_loop(1, peers, hear, 0)
+    each(lambda q: occupancy_copy(q).wait_recv())
     for d in range(n):
         summed = o_in[d * nb + lax.rem(mb + nb, nb)]
         for b in range(1, nb):
@@ -346,12 +360,7 @@
     applied[1] = result[:, bands : 2 * bands]
     for copy in sends + p_sends:
         copy.wait_send()
-
-    def told(q, carry):
-        occupancy_copy(q).wait_send()
-        return carry
-
-    lax.fori_loop(1, peers, told, 0)
+    each(lambda q: occupancy_copy(q).wait_send())
 
 
 def finish(applied_in, onsite_in, applied, onsite, sem):
@@ -418,6 +427,7 @@
                 dma((n,)),
                 dma((n * nb,)),
                 dma((n * nb,)),
+                pltpu.SemaphoreType.REGULAR,
             ],
             compiler_params=pltpu.CompilerParams(
                 collective_id=0, has_side_effects=True, vmem_limit_bytes=40 * 2**20

time: 21 us -> 19.8 us (0.943)
  Pallas kernels: 20.2 us -> 18.9 us
    pallas_call x1, Pallas kernels: 19.4 us -> 18.2 us  [local(): pl.pallas_call(functools.partial(kernel, n, nb), out_shape=results, in_sp...]
where the time goes in v3:
time: 19.8 us; the launch traced here: 19.5 us
  Pallas kernels  18.9 us (95%)
  between operations  0.64 us (3%)
    pallas_call x1, Pallas kernels, local(): pl.pallas_call(functools.partial(kernel, n, nb), out_shape=results, in_sp...  18.2 us
    pallas_call x1, Pallas kernels, local(): pl.pallas_call(finish, out_shape=results, in_specs=[anywhere] * 2, out_sp...  0.72 us

profile of v3, /device:TPU:0, one launch (start us, length us, event | category | flops | bytes accessed | tf_op | source)
XLA Modules:
  0.0 19.5 jit_solution(15402023580188599223)
XLA Ops:
  0.6 18.2 %shard_map.113 = (bf16[2,512,128]{2,1,0:T(8,128)(2,1)S(1)}, f32[4,8,8]{2,1,0:T(8,128)S(1)}) custom-call(bf16[2,512,128]{2,1,0:T(8,128)(2,1)} %wave.1, s32[3,512]{1,0:T(4,128)} %miller_h.1, f32[3,3]{1,0:T(4,128)} %reciprocal_h.1, f32[3,32]{1,0:T(4,128)} %fractional_h.1, s32[32]{0:T(128)} %species_h.1, s32[32]{0:T(128)} %order_h.1, f32[4,4]{1,0:T(4,128)} %widths_h.1, ...), custom_call_target="tpu_custom_call" | custom-call | tf_op jit(solution)/shard_map/pallas_call | solution.py:394
  18.8 0.7 %shard_map.114 = (bf16[2,512,128]{2,1,0:T(8,128)(2,1)}, f32[4,8,8]{2,1,0:T(8,128)}) custom-call(bf16[2,512,128]{2,1,0:T(8,128)(2,1)S(1)} %get-tuple-element.4.applied_in, f32[4,8,8]{2,1,0:T(8,128)S(1)} %get-tuple-element.5.onsite_in), custom_call_target="tpu_custom_call" | custom-call | tf_op jit(solution)/shard_map/pallas_call | solution.py:453
